TPU v7x, 32 devices: a whole 2x2x4 slice. The times are simulated.
32 devices in a mesh: row: 8 (over z, y), col: 4 (over x, core).
Axes of the slice: x: 2, y: 2, z: 4, core: 2. Of those that a mesh axis runs over, the one named last changes fastest.
Arguments:
- image_in: bfloat16 [2048, 1536], P('row', 'col'), may hold values from -6 to 6
- text_in: bfloat16 [2464, 1536], P('row', 'col'), may hold values from -6 to 6
- condition: bfloat16 [16, 1536], P(None, 'row'), may hold values from -6 to 6
- ranges: int32 [16, 2], P('row'), may hold values from 0 to 192, as said below
- mod_weight: bfloat16 [1, 1536, 2, 6, 1536], P(None, 'row', None, None, 'col'), may hold values from -0.15625 to 0.15625
- qkv_weight: bfloat16 [1, 1536, 2, 3, 1536], P(None, 'row', None, None, 'col'), may hold values from -0.15625 to 0.15625
- out_weight: bfloat16 [1, 1536, 2, 1536], P(None, 'row', None, 'col'), may hold values from -2.5 to 2.5
- up_weight: bfloat16 [1, 1536, 2, 6144], P(None, 'row', None, 'col'), may hold values from -0.15625 to 0.15625
- down_weight: bfloat16 [1, 1536, 2, 6144], P(None, 'row', None, 'col'), may hold values from -0.078125 to 0.078125
- image_cot: bfloat16 [2048, 1536], P('row', 'col'), may hold values from -6 to 6
- text_cot: bfloat16 [2464, 1536], P('row', 'col'), may hold values from -6 to 6
Outputs:
- image_out: float32 [2048, 1536], P('row', 'col')
- text_out: float32 [2464, 1536], P('row', 'col')
- grad_image: float32 [2048, 1536], P('row', 'col')
- grad_text: float32 [2464, 1536], P('row', 'col')
- grad_cond: float32 [16, 1536], P(None, 'row')
- grad_mod: float32 [1, 1536, 2, 6, 1536], P(None, 'row', None, None, 'col')
- grad_qkv: float32 [1, 1536, 2, 3, 1536], P(None, 'row', None, None, 'col')
- grad_out: float32 [1, 1536, 2, 1536], P(None, 'row', None, 'col')
- grad_up: float32 [1, 1536, 2, 6144], P(None, 'row', None, 'col')
- grad_down: float32 [1, 1536, 2, 6144], P(None, 'row', None, 'col')
Inputs may be any that keep to these rules, and one draw needn't show every extreme that they name: `ranges`: each index of row has 2 slots; the first always holds 154 text rows and a multiple of 64 image rows; the second is empty or holds 154 text rows and exactly the image rows the first leaves over, so that index's 256 image rows are full.
All inputs are finite; a program needn't handle non-finite values.
Results may differ from a plain program's by a relative error of at most 0.015.
The roundings to bfloat16 on the way count: a program that leaves them out, or rounds other values in their place, can miss the bound.
Values may be sent and summed in bfloat16 or wider, within the bound.
A program may use at most 320 MiB of HBM per device.

v0:
```python
import math
import jax
import jax.numpy as jnp
from jax import lax
from jax.sharding import PartitionSpec as P

D = 1536
LAYERS = 1
IMG_DEV = 256
HD = 64
TXT_DEV = 308
EPSILON = 1e-06
HIGHEST = lax.Precision.HIGHEST


def slot_table(lengths, image_rows, text_rows):
    ends = jnp.cumsum(lengths, axis=0, dtype=jnp.int32)
    starts = ends - lengths
    slot_ids = jnp.arange(lengths.shape[0], dtype=jnp.int32)
    tables = []
    segments = []
    for column, amount in ((0, image_rows), (1, text_rows)):
        places = jnp.arange(amount, dtype=jnp.int32)[:, None]
        inside = ((places >= starts[None, :, column]) & (places < ends[None, :, column])).astype(
            jnp.int32
        )
        tables.append(inside.astype(jnp.float32))
        filled = jnp.sum(inside, axis=1, dtype=jnp.int32)
        segments.append(
            jnp.sum(inside * slot_ids[None, :], axis=1, dtype=jnp.int32)
            + lengths.shape[0] * (1 - filled)
        )
    return (jnp.concatenate(tables, axis=0), jnp.concatenate(segments, axis=0))


def stream_dot(left, right_image, right_text):
    upper = jnp.dot(left[:IMG_DEV], right_image, preferred_element_type=jnp.float32)
    lower = jnp.dot(left[IMG_DEV:], right_text, preferred_element_type=jnp.float32)
    return jnp.concatenate([upper, lower], axis=0)


def stream_outer(left, right):
    upper = jnp.einsum(
        "nk,nf->kf", left[:IMG_DEV], right[:IMG_DEV], preferred_element_type=jnp.float32
    )
    lower = jnp.einsum(
        "nk,nf->kf", left[IMG_DEV:], right[IMG_DEV:], preferred_element_type=jnp.float32
    )
    return (upper, lower)


def row_mod(slot_ones, mod_mine, layer_index, component):
    upper = jnp.dot(slot_ones[:IMG_DEV], mod_mine[:, layer_index, 0, component], precision=HIGHEST)
    lower = jnp.dot(slot_ones[IMG_DEV:], mod_mine[:, layer_index, 1, component], precision=HIGHEST)
    return jnp.concatenate([upper, lower], axis=0)


def slot_sums(slot_ones, rows):
    upper = jnp.dot(slot_ones[:IMG_DEV].T, rows[:IMG_DEV], precision=HIGHEST)
    lower = jnp.dot(slot_ones[IMG_DEV:].T, rows[IMG_DEV:], precision=HIGHEST)
    return jnp.stack([upper, lower], axis=1)


def feature_sums(first, second):
    return lax.psum((jnp.sum(first, axis=1), jnp.sum(second, axis=1)), "col")


def normalize(hidden):
    totals, squares = feature_sums(hidden, hidden * hidden)
    center = totals / D
    spread = squares / D - center * center
    scaling = lax.rsqrt(spread + EPSILON)
    return ((hidden - center[:, None]) * scaling[:, None], scaling[:, None])


def norm_back(grad_hat, normed, scaling):
    first, second = feature_sums(grad_hat, grad_hat * normed)
    return scaling * (grad_hat - first[:, None] / D - normed * (second[:, None] / D))


def gelu_slope(value):
    coeff = math.sqrt(2.0 / math.pi)
    tangent = jnp.tanh(coeff * (value + 0.044715 * value * value * value))
    return 0.5 * (1.0 + tangent) + 0.5 * value * (1.0 - tangent * tangent) * coeff * (
        1.0 + 3.0 * 0.044715 * value * value
    )


def silu_slope(value):
    sigma = jax.nn.sigmoid(value)
    return sigma * (1.0 + value * (1.0 - sigma))


def gather_features(values):
    return lax.all_gather(values, "col", axis=1, tiled=True)


def gather_grads(values):
    return lax.all_gather(values, "col", axis=1, tiled=True)


def scatter_features(values):
    return lax.psum_scatter(values, "col", scatter_dimension=1, tiled=True)


def scatter_back(values):
    return lax.psum_scatter(values, "col", scatter_dimension=1, tiled=True)


def spread_grads(terms, row_count):
    return lax.psum_scatter(
        terms(jnp.int32(0), row_count * lax.axis_size("row")),
        "row",
        scatter_dimension=0,
        tiled=True,
    )


def fold_rows(left, weight):
    portion = lax.all_gather(weight, "row", axis=0, tiled=True)
    return stream_dot(left, portion[:, 0], portion[:, 1])


def map_rows(left, weight):
    portion = lax.all_gather(weight, "row", axis=0, tiled=True)
    return stream_dot(left, portion[:, 0].T, portion[:, 1].T)


def apply_in(left, weight):
    result = fold_rows(left, weight)
    return result


def apply_out(left, weight):
    result = map_rows(left, weight)
    return result


def mlp_part(operands):
    grad_full, gathered, grad_lifted, activated = operands
    up_image, up_text = stream_outer(gathered, grad_lifted)
    down_image, down_text = stream_outer(grad_full, activated)
    image_part = jnp.concatenate([up_image, down_image], axis=1)
    text_part = jnp.concatenate([up_text, down_text], axis=1)
    return jnp.stack([image_part, text_part], axis=1)


def attention_part(operands):
    grad_full, gathered, grad_projected, mixed = operands
    qkv_image, qkv_text = stream_outer(gathered, grad_projected)
    out_image, out_text = stream_outer(grad_full, mixed)
    image_part = jnp.concatenate([qkv_image, out_image], axis=1)
    text_part = jnp.concatenate([qkv_text, out_text], axis=1)
    return jnp.stack([image_part, text_part], axis=1)


def attend_head(operands, segments, scale):
    queries, key_rows, value_rows = operands
    scores = jnp.dot(queries, key_rows.T, preferred_element_type=jnp.float32) * scale
    allowed = segments[:, None] == segments[None, :]
    scores = jnp.where(allowed, scores, -jnp.inf)
    highest = jnp.max(scores, axis=1, keepdims=True)
    log_total = highest + jnp.log(jnp.sum(jnp.exp(scores - highest), axis=1, keepdims=True))
    weights = jnp.exp(scores - log_total).astype(jnp.bfloat16)
    output = jnp.dot(weights, value_rows, preferred_element_type=jnp.float32).astype(jnp.bfloat16)
    return (output, log_total[:, 0])


def attend_back_head(operands, segments, scale):
    queries, key_rows, value_rows, output, grad_output, log_total = operands
    scores = jnp.dot(queries, key_rows.T, preferred_element_type=jnp.float32) * scale
    allowed = segments[:, None] == segments[None, :]
    scores = jnp.where(allowed, scores, -jnp.inf)
    probs = jnp.exp(scores - log_total[:, None])
    grad_values = jnp.dot(
        probs.astype(jnp.bfloat16).T, grad_output, preferred_element_type=jnp.float32
    )
    grad_probs = jnp.dot(grad_output, value_rows.T, preferred_element_type=jnp.float32)
    inner = jnp.sum(
        grad_output.astype(jnp.float32) * output.astype(jnp.float32), axis=1, keepdims=True
    )
    grad_scores = (probs * (grad_probs - inner) * scale).astype(jnp.bfloat16)
    grad_queries = jnp.dot(grad_scores, key_rows, preferred_element_type=jnp.float32)
    grad_keys = jnp.dot(grad_scores.T, queries, preferred_element_type=jnp.float32)
    return jnp.stack([grad_queries, grad_keys, grad_values], axis=0).astype(jnp.bfloat16)


def per_device(
    image_in,
    text_in,
    condition,
    ranges,
    mod_weight,
    qkv_weight,
    out_weight,
    up_weight,
    down_weight,
    image_cot,
    text_cot,
):
    slot_ones, segments = slot_table(ranges, IMG_DEV, TXT_DEV)
    col_width = image_in.shape[1]
    ff_width = up_weight.shape[3]
    row_count = qkv_weight.shape[1]
    heads_here = col_width // HD
    scale = 1.0 / math.sqrt(HD)
    silu_cond = jax.nn.silu(condition.astype(jnp.float32)).astype(jnp.bfloat16)
    mod_terms = jnp.einsum(
        "sd,ldxkf->slxkf", silu_cond, mod_weight, preferred_element_type=jnp.float32
    )
    mod_mine = lax.psum_scatter(mod_terms, "row", scatter_dimension=0, tiled=True)
    hidden = jnp.concatenate([image_in, text_in], axis=0).astype(jnp.float32)
    layer_index = 0
    qkv_local = qkv_weight[layer_index].reshape(row_count, 2, 3 * col_width)
    whole = (None, None, None, None)
    mods = [row_mod(slot_ones, mod_mine, layer_index, part_no) for part_no in range(6)]
    normed_one, scaling_one = normalize(hidden)
    modulated_one = (normed_one * (1.0 + mods[1]) + mods[0]).astype(jnp.bfloat16)
    gathered_one = gather_features(modulated_one)
    projected = apply_in(gathered_one, qkv_local).astype(jnp.bfloat16)
    heads_form = projected.reshape(-1, 3, heads_here, HD).transpose(1, 2, 0, 3)
    attended, log_totals = lax.map(
        lambda operands: attend_head(operands, segments, scale),
        (heads_form[0], heads_form[1], heads_form[2]),
    )
    mixed = attended.transpose(1, 0, 2).reshape(-1, col_width)
    branch_one = scatter_features(apply_out(mixed, out_weight[layer_index]))
    midway = hidden + mods[2] * branch_one
    normed_two, scaling_two = normalize(midway)
    modulated_two = (normed_two * (1.0 + mods[4]) + mods[3]).astype(jnp.bfloat16)
    gathered_two = gather_features(modulated_two)
    lifted = apply_in(gathered_two, up_weight[layer_index])
    activated = jax.nn.gelu(lifted, approximate=True).astype(jnp.bfloat16)
    branch_two = scatter_features(apply_out(activated, down_weight[layer_index]))
    hidden = midway + mods[5] * branch_two
    saved = [
        (
            whole,
            normed_one,
            scaling_one,
            gathered_one,
            heads_form,
            attended,
            log_totals,
            mixed,
            branch_one,
            normed_two,
            scaling_two,
            gathered_two,
            lifted,
            activated,
            branch_two,
        )
    ]
    image_out = hidden[:IMG_DEV]
    text_out = hidden[IMG_DEV:]
    grad_hidden = jnp.concatenate([image_cot, text_cot], axis=0).astype(jnp.float32)
    grads_qkv = [None] * LAYERS
    grads_out = [None] * LAYERS
    grads_up = [None] * LAYERS
    grads_down = [None] * LAYERS
    grads_slots = [None] * LAYERS
    for layer_index in reversed(range(LAYERS)):
        (
            whole,
            normed_one,
            scaling_one,
            gathered_one,
            heads_form,
            attended,
            log_totals,
            mixed,
            branch_one,
            normed_two,
            scaling_two,
            gathered_two,
            lifted,
            activated,
            branch_two,
        ) = saved[layer_index]
        qkv_local = qkv_weight[layer_index].reshape(row_count, 2, 3 * col_width)
        mods = [row_mod(slot_ones, mod_mine, layer_index, part_no) for part_no in range(6)]
        grad_branch_two = (grad_hidden * mods[5]).astype(jnp.bfloat16)
        gate_two_rows = grad_hidden * branch_two
        grad_full_two = gather_grads(grad_branch_two)
        grad_act = apply_in(grad_full_two, down_weight[layer_index])
        grad_lifted = (grad_act * gelu_slope(lifted)).astype(jnp.bfloat16)
        mlp_operands = (grad_full_two, gathered_two, grad_lifted, activated)
        mlp_grads = spread_grads(lambda offset, amount: mlp_part(mlp_operands), row_count)
        grads_up[layer_index] = mlp_grads[:, :, :ff_width]
        grads_down[layer_index] = mlp_grads[:, :, ff_width:]
        grad_mod_two = scatter_back(apply_out(grad_lifted, up_weight[layer_index]))
        scale_two_rows = grad_mod_two * normed_two
        grad_hidden = grad_hidden + norm_back(
            grad_mod_two * (1.0 + mods[4]), normed_two, scaling_two
        )
        grad_branch_one = (grad_hidden * mods[2]).astype(jnp.bfloat16)
        gate_one_rows = grad_hidden * branch_one
        grad_full_one = gather_grads(grad_branch_one)
        grad_mixed = apply_in(grad_full_one, out_weight[layer_index]).astype(jnp.bfloat16)
        grad_heads = grad_mixed.reshape(-1, heads_here, HD).transpose(1, 0, 2)
        grad_parts = lax.map(
            lambda operands: attend_back_head(operands, segments, scale),
            (heads_form[0], heads_form[1], heads_form[2], attended, grad_heads, log_totals),
        )
        grad_projected = grad_parts.transpose(2, 1, 0, 3).reshape(-1, 3 * col_width)
        attention_operands = (grad_full_one, gathered_one, grad_projected, mixed)
        attention_grads = spread_grads(
            lambda offset, amount: attention_part(attention_operands), row_count
        )
        grads_qkv[layer_index] = attention_grads[:, :, : 3 * col_width].reshape(
            row_count, 2, 3, col_width
        )
        grads_out[layer_index] = attention_grads[:, :, 3 * col_width :]
        grad_mod_one = scatter_back(apply_out(grad_projected, qkv_local))
        scale_one_rows = grad_mod_one * normed_one
        grad_hidden = grad_hidden + norm_back(
            grad_mod_one * (1.0 + mods[1]), normed_one, scaling_one
        )
        rows_list = [
            grad_mod_one,
            scale_one_rows,
            gate_one_rows,
            grad_mod_two,
            scale_two_rows,
            gate_two_rows,
        ]
        grads_slots[layer_index] = jnp.stack(
            [slot_sums(slot_ones, rows) for rows in rows_list], axis=2
        )
    mod_all = lax.all_gather(jnp.stack(grads_slots, axis=1), "row", axis=0, tiled=True)
    grad_mod = jnp.einsum(
        "sd,slxkf->ldxkf", silu_cond.astype(jnp.float32), mod_all, precision=HIGHEST
    )
    cond_part = jnp.einsum(
        "slxkf,ldxkf->sd", mod_all, mod_weight.astype(jnp.float32), precision=HIGHEST
    )
    cond_total = lax.psum(cond_part, "col")
    grad_cond = cond_total * silu_slope(condition.astype(jnp.float32))
    grad_image = grad_hidden[:IMG_DEV]
    grad_text = grad_hidden[IMG_DEV:]
    return (
        image_out,
        text_out,
        grad_image,
        grad_text,
        grad_cond,
        grad_mod,
        jnp.stack(grads_qkv),
        jnp.stack(grads_out),
        jnp.stack(grads_up),
        jnp.stack(grads_down),
    )


def solution(mesh):
    return jax.shard_map(
        per_device,
        mesh=mesh,
        in_specs=(
            P("row", "col"),
            P("row", "col"),
            P(None, "row"),
            P("row", None),
            P(None, "row", None, None, "col"),
            P(None, "row", None, None, "col"),
            P(None, "row", None, "col"),
            P(None, "row", None, "col"),
            P(None, "row", None, "col"),
            P("row", "col"),
            P("row", "col"),
        ),
        out_specs=(
            P("row", "col"),
            P("row", "col"),
            P("row", "col"),
            P("row", "col"),
            P(None, "row"),
            P(None, "row", None, None, "col"),
            P(None, "row", None, None, "col"),
            P(None, "row", None, "col"),
            P(None, "row", None, "col"),
            P(None, "row", None, "col"),
        ),
        check_vma=False,
    )
```

profile of v0, /device:TPU:0, one launch (start us, length us, event | category | flops | bytes accessed | tf_op | source)
XLA Modules:
  0.0 2627.9 jit_solution(4866509215842069157)
XLA Ops:
  15.9 8.5 all-reduce.6
  24.7 61.2 %all-reduce.11.cloned.1.call-done = f32[16,1,2,6,384]{4,0,3,2,1:T(8,128)} async-done(((f32[16,1,2,6,384]{4,0,3,2,1:T(8,128)}), f32[16,1,2,6,384]{4,0,3,2,1:T(8,128)}) %all-reduce.11.cloned.1.call-update) | async-done | bytes 294928
  95.3 100.8 %all-gather.15.cloned.1.call-done = bf16[1536,2,1152]{2,0,1:T(8,128)(2,1)} async-done(((bf16[192,2,1152]{2,0,1:T(8,128)(2,1)}), bf16[1536,2,1152]{2,0,1:T(8,128)(2,1)}) %all-gather.15.cloned.1.call-update) | async-done | bytes 7077904 | tf_op jit(solution)/shard_map/all_gather | solution.py:120
  196.0 6.6 slice_bitcast_fusion.13
  202.6 5.8 copy.120
  208.4 5.8 copy.119
  229.1 16.3 while.22
  249.0 22.4 all-gather.23.cloned.1.call-done
  297.1 17.9 reduce-scatter.6.cloned.1.call-done
  316.8 5.9 all-reduce.5
  325.0 12.6 all-gather.19.cloned.1.call-done
  337.6 140.0 %all-gather.27.cloned.1.call-done = bf16[1,1536,2,1536]{3,1,2,0:T(8,128)(2,1)} async-done(((bf16[1,192,2,1536]{3,1,2,0:T(8,128)(2,1)}), bf16[1,1536,2,1536]{3,1,2,0:T(8,128)(2,1)}) %all-gather.27.cloned.1.call-update) | async-done | bytes 9437200 | tf_op jit(solution)/shard_map/all_gather | solution.py:125
  488.2 127.7 %all-gather.25.cloned.1.call-done = bf16[1,1536,2,1536]{3,1,2,0:T(8,128)(2,1)} async-done(((bf16[1,192,2,1536]{3,1,2,0:T(8,128)(2,1)}), bf16[1,1536,2,1536]{3,1,2,0:T(8,128)(2,1)}) %all-gather.25.cloned.1.call-update) | async-done | bytes 9437200 | tf_op jit(solution)/shard_map/all_gather | solution.py:120
  615.9 20.9 all-gather.17.cloned.1.call-done
  665.1 29.2 %reduce-scatter.10.cloned.1.call-done = f32[564,384]{1,0:T(8,128)} async-done(((f32[564,1536]{1,0:T(8,128)}), f32[564,384]{1,0:T(8,128)}) %reduce-scatter.10.cloned.1.call-update) | async-done | bytes 866320 | tf_op jit(solution)/shard_map/reduce_scatter | solution.py:107
  696.2 6.4 all-reduce.4
  703.3 34.0 %reduce-scatter.8.cloned.1.call-done = f32[564,384]{1,0:T(8,128)} async-done(((f32[564,1536]{1,0:T(8,128)}), f32[564,384]{1,0:T(8,128)}) %reduce-scatter.8.cloned.1.call-update) | async-done | bytes 866320 | tf_op jit(solution)/shard_map/reduce_scatter | solution.py:103
  743.6 9.1 reduce-scatter.12.cloned.1.call-start
  769.1 64.8 %while.23 = (s32[]{:T(128)}, bf16[6,3,564,64]{2,3,0,1:T(8,128)(2,1)}, s32[564]{0:T(1024)}, bf16[6,564,64]{2,1,0:T(8,128)(2,1)}, bf16[6,564,64]{2,1,0:T(8,128)(2,...) while((s32[]{:T(128)}, ...), condition=%wide.region_27.28_spmd, body=%wide.region_25.27_spmd.sunk | while | flops 207346144 | bytes 8018613 | solution.py:302
  859.0 8.2 maximum_bitcast_fusion.4
  867.3 7.8 maximum_bitcast_fusion.3
  875.0 14.7 pad_maximum_fusion.1
  889.7 28.5 %copy.139 = f32[1536,2,1536]{2,1,0:T(2,128)} copy(f32[1536,2,1536]{0,2,1:T(8,128)} %pad_maximum_fusion.1) | data formatting | bytes 37748736 | tf_op jit(solution)/shard_map/stack | solution.py:154
  937.3 7.8 maximum_bitcast_fusion.2
  945.1 11.3 maximum_bitcast_fusion.1
  956.4 21.2 pad_maximum_fusion
  977.5 55.5 %copy.141 = f32[1536,2,3072]{2,1,0:T(2,128)} copy(f32[1536,2,3072]{0,2,1:T(8,128)} %pad_maximum_fusion) | data formatting | bytes 75497472 | tf_op jit(solution)/shard_map/stack | solution.py:145
  1054.0 33.8 %all-gather.3 = f32[16,2,6,384]{3,1,2,0:T(2,128)S(1)} all-gather(f32[2,2,6,384]{3,1,2,0:T(2,128)S(1)} %copy.135), channel_id=5, replica_groups=mesh['row'=8,'col'=4] {'row'}, dimensions={0}, use_global_device_ids=true | all-gather | bytes 331776 | tf_op jit(solution)/shard_map/all_gather | solution.py:331
  1090.0 11.9 all-reduce.3
  1112.1 376.4 %all-reduce.13.cloned.1.call-done = f32[1536,2,1536]{2,1,0:T(2,128)} async-done(((f32[1536,2,1536]{2,1,0:T(2,128)}), f32[1536,2,1536]{2,1,0:T(2,128)}) %all-reduce.13.cloned.1.call-update) | async-done | bytes 18874384
  1494.4 1118.8 %all-reduce.15.cloned.1.call-done = f32[1536,2,3072]{2,1,0:T(2,128)} async-done(((f32[1536,2,3072]{2,1,0:T(2,128)}), f32[1536,2,3072]{2,1,0:T(2,128)}) %all-reduce.15.cloned.1.call-update) | async-done | bytes 37748752
  2613.2 7.8 dynamic-slice_bitcast_fusion
  (387 shorter events, 292.2 us)
Async XLA Ops:
  7.2 78.7 %all-reduce.11.cloned.1.call-start = ((), (), s32[]{:S(2)}) async-start(), calls=%async_computation.16 | async-start | bytes 589824
  10.5 185.5 %all-gather.15.cloned.1.call-start = ((), (), s32[]{:S(2)}) async-start(), calls=%async_computation.5 | async-start | bytes 7962624 | tf_op jit(solution)/shard_map/all_gather | solution.py:120
  14.3 202.7 %all-gather.13.cloned.1.call-start = ((), (), s32[]{:S(2)}) async-start(), calls=%async_computation.4 | async-start | bytes 2181120 | tf_op jit(solution)/shard_map/all_gather | solution.py:95
  24.6 264.2 %copy-start.45 = (s32[2]{0:T(128)}, s32[2]{0:T(128)S(1)}, u32[]{:S(2)}) copy-start(s32[2]{0:T(128)S(1)} %get-tuple-element.240) | copy-start | bytes 28
  24.7 264.2 %copy-start.47 = (s32[2]{0:T(128)}, s32[2]{0:T(128)S(1)}, u32[]{:S(2)}) copy-start(s32[2]{0:T(128)S(1)} %get-tuple-element.315) | copy-start | bytes 28
  24.7 270.1 %copy-start.49 = (s32[2]{0:T(128)}, s32[2]{0:T(128)S(1)}, u32[]{:S(2)}) copy-start(s32[2]{0:T(128)S(1)} %get-tuple-element.241) | copy-start | bytes 28
  24.7 270.1 %copy-start.51 = (s32[2]{0:T(128)}, s32[2]{0:T(128)S(1)}, u32[]{:S(2)}) copy-start(s32[2]{0:T(128)S(1)} %get-tuple-element.314) | copy-start | bytes 28
  24.7 68.8 %copy-start.54 = (f32[564]{0:T(1024)}, f32[564]{0:T(1024)S(1)}, u32[]{:S(2)}) copy-start(f32[564]{0:T(1024)S(1)} %get-tuple-element.312) | copy-start | bytes 6772
  24.7 68.8 %copy-start.56 = (f32[564]{0:T(1024)}, f32[564]{0:T(1024)S(1)}, u32[]{:S(2)}) copy-start(f32[564]{0:T(1024)S(1)} %get-tuple-element.313) | copy-start | bytes 6772
  93.6 177.9 %all-gather.23.cloned.1.call-start = ((), (), s32[]{:S(2)}) async-start(), calls=%async_computation.13 | async-start | bytes 2654208 | tf_op jit(solution)/shard_map/all_gather | solution.py:125
  94.4 220.6 %reduce-scatter.6.cloned.1.call-start = ((), (), s32[]{:S(2)}) async-start(), calls=%async_computation.6 | async-start | bytes 4362240 | tf_op jit(solution)/shard_map/reduce_scatter | solution.py:103
  245.4 28.9 %copy-start.17 = (bf16[6,564,64]{2,1,0:T(8,128)(2,1)}, bf16[6,564,64]{2,1,0:T(8,128)(2,1)S(1)}, u32[]{:S(2)}) copy-start(bf16[6,564,64]{2,1,0:T(8,128)(2,1)S(1)} %get-tuple-element.510) | copy-start | bytes 1299460
  245.4 28.9 %copy-start.28 = (bf16[6,564,64]{2,1,0:T(8,128)(2,1)}, bf16[6,564,64]{2,1,0:T(8,128)(2,1)S(1)}, u32[]{:S(2)}) copy-start(bf16[6,564,64]{2,1,0:T(8,128)(2,1)S(1)} %get-tuple-element.518) | copy-start | bytes 1299460
  276.4 61.2 %all-gather.19.cloned.1.call-start = ((), (), s32[]{:S(2)}) async-start(), calls=%async_computation.9 | async-start | bytes 2181120 | tf_op jit(solution)/shard_map/all_gather | solution.py:99
  281.5 196.2 %all-gather.27.cloned.1.call-start = ((), (), s32[]{:S(2)}) async-start(), calls=%async_computation.15 | async-start | bytes 10616832 | tf_op jit(solution)/shard_map/all_gather | solution.py:125
  282.7 333.2 %all-gather.25.cloned.1.call-start = ((), (), s32[]{:S(2)}) async-start(), calls=%async_computation.14 | async-start | bytes 10616832 | tf_op jit(solution)/shard_map/all_gather | solution.py:120
  285.5 351.3 %all-gather.17.cloned.1.call-start = ((), (), s32[]{:S(2)}) async-start(), calls=%async_computation.7 | async-start | bytes 2181120 | tf_op jit(solution)/shard_map/all_gather | solution.py:95
  288.9 33.8 %copy-start.14 = (f32[256,384]{1,0:T(8,128)}, f32[256,384]{1,0:T(8,128)S(1)}, u32[]{:S(2)}) copy-start(f32[256,384]{1,0:T(8,128)S(1)} %fusion.196) | copy-start | bytes 1179652
  294.8 30.1 %copy-start.7 = (f32[308,384]{1,0:T(8,128)}, f32[308,384]{1,0:T(8,128)S(1)}, u32[]{:S(2)}) copy-start(f32[308,384]{1,0:T(8,128)S(1)} %fusion.163) | copy-start | bytes 1419268
  325.0 369.3 %reduce-scatter.10.cloned.1.call-start = ((), (), s32[]{:S(2)}) async-start(), calls=%async_computation.10 | async-start | bytes 4362240 | tf_op jit(solution)/shard_map/reduce_scatter | solution.py:107
  654.2 83.1 %reduce-scatter.8.cloned.1.call-start = ((), (), s32[]{:S(2)}) async-start(), calls=%async_computation.8 | async-start | bytes 4362240 | tf_op jit(solution)/shard_map/reduce_scatter | solution.py:103
  665.1 99.2 %all-gather.21.cloned.1.call-start = ((), (), s32[]{:S(2)}) async-start(), calls=%async_computation.11 | async-start | bytes 2181120 | tf_op jit(solution)/shard_map/all_gather | solution.py:99
  694.3 43.1 %copy-start.4 = (f32[564,384]{1,0:T(8,128)S(1)}, f32[564,384]{1,0:T(8,128)}, u32[]{:S(2)}) copy-start(f32[564,384]{1,0:T(8,128)} %reduce-scatter.10.cloned.1.call-done) | copy-start | bytes 2598916
  743.6 304.8 %reduce-scatter.12.cloned.1.call-start = ((), (), s32[]{:S(2)}) async-start(), calls=%async_computation.12 | async-start | bytes 4362240 | tf_op jit(solution)/shard_map/reduce_scatter | solution.py:107
  845.6 642.9 %all-reduce.13.cloned.1.call-start = ((), (), s32[]{:S(2)}) async-start(), calls=%async_computation.17 | async-start | bytes 37748736
  918.3 1694.9 %all-reduce.15.cloned.1.call-start = ((), (), s32[]{:S(2)}) async-start(), calls=%async_computation.18 | async-start | bytes 75497472
  1035.8 15.3 copy-start.9
  1035.8 15.3 copy-start.16
  1035.8 15.4 copy-start.55
  1035.8 15.4 copy-start.57
  1053.1 48.8 %copy-start.3 = (f32[564,384]{1,0:T(8,128)S(1)}, f32[564,384]{1,0:T(8,128)}, u32[]{:S(2)}) copy-start(f32[564,384]{1,0:T(8,128)} %copy-done.2) | copy-start | bytes 2598916
  1053.1 48.8 %copy-start.6 = (f32[564,384]{1,0:T(8,128)S(1)}, f32[564,384]{1,0:T(8,128)}, u32[]{:S(2)}) copy-start(f32[564,384]{1,0:T(8,128)} %reduce-scatter.12.cloned.1.call-done) | copy-start | bytes 2598916
  (51 other events, 202.1 us)
Sparse Core Ops, SparseCore 0:
  11.9 73.9 all-reduce.10
  88.7 107.3 all-gather.14
  198.2 18.7 all-gather.12
  219.6 51.8 all-gather.22
  276.5 38.4 reduce-scatter.5
  317.0 20.5 all-gather.18
  340.4 137.2 all-gather.26
  480.4 135.4 all-gather.24
  618.0 18.7 all-gather.16
  654.3 39.8 reduce-scatter.9
  697.4 39.8 reduce-scatter.7
  743.7 20.5 all-gather.20
  845.7 39.8 reduce-scatter.11
  918.4 570.0 all-reduce.12
  1492.6 1120.5 all-reduce.14
where the time goes:
time: 2640 us; the launch traced here: 2630 us
  waiting for transfers between devices  2070 us (78%)
  local copies, waits for them, and re-layouts  178 us (7%)
  matrix products  171 us (6%)
  other arithmetic  116 us (4%)
  blocking collectives  66.6 us (3%)
    unnamed x18, waiting for transfers between devices  1560 us
    all_gather x2, waiting for transfers between devices, fold_rows(): portion = lax.all_gather(weight, 'row', axis=0, tiled=True)  228 us
    all_gather x2, waiting for transfers between devices, map_rows(): portion = lax.all_gather(weight, 'row', axis=0, tiled=True)  162 us
    another operation x1, local copies, waits for them, and re-layouts, mlp_part(): return jnp.stack([image_part, text_part], axis=1)  55.5 us
  transfers between devices with their start and end apart: 15, of which 14 were waited for; matrix products, arithmetic and copies ran while one was open for 13% of the time, Pallas kernels for 0%

commit v1 on v0

--- a/solution.py
+++ b/solution.py
@@ -11,6 +11,34 @@
 TXT_DEV = 308
 EPSILON = 1e-06
 HIGHEST = lax.Precision.HIGHEST
+
+
+def ends_track(local_x, in_dim):
+    left_arr = list(local_x.shape[1:])
+    left_arr[in_dim] *= local_x.shape[0]
+    f_next = jnp.moveaxis(local_x, 0, in_dim).reshape(left_arr)
+    return f_next
+
+
+def _track_squares(row_axis, local_values, d_out=0):
+    world_n = lax.axis_size(row_axis)
+    series = [(i, (i + 1) % world_n) for i in range(world_n)]
+    vals = [(rr, p) for p, rr in series]
+    part_next, wide_out = ([], [])
+    for j in tuple(range(world_n - 1)):
+        if j % 2 == 0:
+            new = lax.ppermute(part_next[-1] if part_next else local_values, row_axis, series)
+            part_next.append(new)
+        else:
+            r2 = lax.ppermute(wide_out[-1] if wide_out else local_values, row_axis, vals)
+            wide_out.append(r2)
+    seen_now = jnp.stack([*part_next[::-1], local_values, *wide_out])
+    after = lax.axis_index(row_axis)
+    z_new = len(part_next)
+    passed = after - z_new
+    seen_now = seen_now[(jnp.arange(world_n) - passed) % world_n]
+    small = ends_track(seen_now, d_out)
+    return small
 
 
 def slot_table(lengths, image_rows, text_rows):
@@ -122,7 +150,7 @@
 
 
 def map_rows(left, weight):
-    portion = lax.all_gather(weight, "row", axis=0, tiled=True)
+    portion = _track_squares("row", weight)
     return stream_dot(left, portion[:, 0].T, portion[:, 1].T)
 
 

time: 2640 us -> 3050 us (1.16)
  local copies, waits for them, and re-layouts: 178 us -> 361 us
  waiting for transfers between devices: 2070 us -> 2220 us
  starting transfers between devices: 10.2 us -> 95.5 us
    ppermute x0 -> x28, waiting for transfers between devices: none -> 495 us  [the longest x16 365 us: _track_squares(): lax.ppermute(part_next[-1] if part_next else local_values, row_axis, series)]
    all_gather x2 -> x0, waiting for transfers between devices: 162 us -> none  [map_rows(): portion = lax.all_gather(weight, 'row', axis=0, tiled=True)]
    ppermute x0 -> x28, starting transfers between devices: none -> 94.4 us  [the longest x12 66.2 us: _track_squares(): lax.ppermute(wide_out[-1] if wide_out else local_values, row_axis, vals)]
    gather x0 -> x8, local copies, waits for them, and re-layouts: none -> 93.2 us  [_track_squares(): seen_now = seen_now[(jnp.arange(world_n) - passed) % world_n]]
    all_gather x2 -> x4, waiting for transfers between devices: 228 us -> 144 us  [fold_rows(): portion = lax.all_gather(weight, 'row', axis=0, tiled=True)]
    unnamed x142 -> x172, local copies, waits for them, and re-layouts: 17.7 us -> 82.8 us
    reduce_scatter x2, waiting for transfers between devices: 51.9 us -> 0.02 us  [scatter_features(): return lax.psum_scatter(values, 'col', scatter_dimension=1, tiled=True)]
  transfers between devices with their start and end apart: 15 -> 43, of which waited for: 14 -> 23; matrix products, arithmetic and copies ran while one was open for 13% -> 16% of each run, Pallas kernels for 0% -> 0%
where the time goes in v1:
time: 3050 us; the launch traced here: 3040 us
  waiting for transfers between devices  2220 us (73%)
  local copies, waits for them, and re-layouts  361 us (12%)
  matrix products  165 us (5%)
  other arithmetic  117 us (4%)
  starting transfers between devices  95.5 us (3%)
  blocking collectives  64.6 us (2%)
    unnamed x18, waiting for transfers between devices  1560 us
    ppermute x16, waiting for transfers between devices, _track_squares(): lax.ppermute(part_next[-1] if part_next else local_values, row_axis, series)  365 us
    all_gather x4, waiting for transfers between devices, fold_rows(): portion = lax.all_gather(weight, 'row', axis=0, tiled=True)  144 us
    ppermute x12, waiting for transfers between devices, _track_squares(): lax.ppermute(wide_out[-1] if wide_out else local_values, row_axis, vals)  130 us
    gather x8, local copies, waits for them, and re-layouts, _track_squares(): seen_now = seen_now[(jnp.arange(world_n) - passed) % world_n]  93.2 us
    unnamed x172, local copies, waits for them, and re-layouts  82.8 us
    ppermute x12, starting transfers between devices, _track_squares(): lax.ppermute(wide_out[-1] if wide_out else local_values, row_axis, vals)  66.2 us
  transfers between devices with their start and end apart: 43, of which 23 were waited for; matrix products, arithmetic and copies ran while one was open for 16% of the time, Pallas kernels for 0%

profile of v1, /device:TPU:0, one launch (start us, length us, event | category | flops | bytes accessed | tf_op | source)
XLA Modules:
  0.0 3041.3 jit_solution(1552610614651062959)
XLA Ops:
  33.8 62.4 %all-reduce.11.cloned.1.call-done = f32[16,1,2,6,384]{4,0,3,2,1:T(8,128)} async-done(((f32[16,1,2,6,384]{4,0,3,2,1:T(8,128)}), f32[16,1,2,6,384]{4,0,3,2,1:T(8,128)}) %all-reduce.11.cloned.1.call-update) | async-done | bytes 294928
  105.4 12.7 collective-permute-done.2
  159.7 52.9 %all-gather.15.cloned.1.call-done = bf16[1536,2,1152]{2,0,1:T(8,128)(2,1)} async-done(((bf16[192,2,1152]{2,0,1:T(8,128)(2,1)}), bf16[1536,2,1152]{2,0,1:T(8,128)(2,1)}) %all-gather.15.cloned.1.call-update) | async-done | bytes 7077904 | tf_op jit(solution)/shard_map/all_gather | solution.py:148
  245.7 23.8 while.22
  287.5 29.1 collective-permute-done.14
  321.3 59.5 %collective-permute-done.15 = bf16[192,2,1536]{2,1,0:T(2,128)(2,1)} collective-permute-done((bf16[192,2,1536]{2,1,0:T(2,128)(2,1)S(1)}, bf16[192,2,1536]{2,1,0:T(2,128)(2,1)}, u32[]{:S(2)}, u32[]{:S(2)}) %collective-permute-start.15) | collective-permute-done | bytes 1179680 | tf_op jit(solution)/shard_map/ppermute | solution.py:30
  385.6 45.9 %collective-permute-done.7 = bf16[192,2,1536]{2,1,0:T(2,128)(2,1)} collective-permute-done((bf16[192,2,1536]{2,1,0:T(2,128)(2,1)}, bf16[192,2,1536]{2,1,0:T(2,128)(2,1)}, u32[]{:S(2)}, u32[]{:S(2)}) %collective-permute-start.7) | collective-permute-done | bytes 1179680 | tf_op jit(solution)/shard_map/ppermute | solution.py:30
  436.2 69.7 %collective-permute-done.16 = bf16[192,2,1536]{2,1,0:T(2,128)(2,1)} collective-permute-done((bf16[192,2,1536]{2,1,0:T(2,128)(2,1)}, bf16[192,2,1536]{2,1,0:T(2,128)(2,1)}, u32[]{:S(2)}, u32[]{:S(2)}) %collective-permute-start.16) | collective-permute-done | bytes 1179680 | tf_op jit(solution)/shard_map/ppermute | solution.py:30
  519.9 36.6 %collective-permute-done.8 = bf16[192,2,1536]{2,1,0:T(2,128)(2,1)} collective-permute-done((bf16[192,2,1536]{2,1,0:T(2,128)(2,1)}, bf16[192,2,1536]{2,1,0:T(2,128)(2,1)}, u32[]{:S(2)}, u32[]{:S(2)}) %collective-permute-start.8) | collective-permute-done | bytes 1179680 | tf_op jit(solution)/shard_map/ppermute | solution.py:30
  559.0 52.1 %collective-permute-done.19 = bf16[192,2,1536]{2,1,0:T(2,128)(2,1)} collective-permute-done((bf16[192,2,1536]{2,1,0:T(2,128)(2,1)}, bf16[192,2,1536]{2,1,0:T(2,128)(2,1)}, u32[]{:S(2)}, u32[]{:S(2)}) %collective-permute-start.19) | collective-permute-done | bytes 1179680 | tf_op jit(solution)/shard_map/ppermute | solution.py:33
  639.5 22.2 collective-permute-done.20
  664.8 24.4 gather_fusion.2
  709.0 91.4 %all-gather.23.cloned.1.call-done = bf16[1,1536,2,1536]{3,1,2,0:T(8,128)(2,1)} async-done(((bf16[1,192,2,1536]{3,1,2,0:T(8,128)(2,1)}), bf16[1,1536,2,1536]{3,1,2,0:T(8,128)(2,1)}) %all-gather.23.cloned.1.call-update) | async-done | bytes 9437200 | tf_op jit(solution)/shard_map/all_gather | solution.py:148
  800.4 20.9 all-gather.17.cloned.1.call-done
  843.6 49.3 %collective-permute-done.12 = bf16[192,2,1536]{2,1,0:T(2,128)(2,1)S(1)} collective-permute-done((bf16[192,2,1536]{2,1,0:T(2,128)(2,1)}, bf16[192,2,1536]{2,1,0:T(2,128)(2,1)S(1)}, u32[]{:S(2)}, u32[]{:S(2)}) %collective-permute-start.12) | collective-permute-done | bytes 1179680 | tf_op jit(solution)/shard_map/ppermute | solution.py:33
  922.2 24.6 gather_fusion.1
  967.6 22.4 collective-permute-done.21
  995.7 31.5 %collective-permute-done.22 = bf16[192,2,1152]{2,0,1:T(8,128)(2,1)} collective-permute-done((bf16[192,2,1152]{2,0,1:T(8,128)(2,1)S(1)}, bf16[192,2,1152]{2,0,1:T(8,128)(2,1)}, u32[]{:S(2)}, u32[]{:S(2)}) %collective-permute-start.22) | collective-permute-done | bytes 884768 | tf_op jit(solution)/shard_map/ppermute | solution.py:30
  1031.6 14.5 collective-permute-start.26
  1046.1 24.5 collective-permute-done.23
  1076.4 22.6 collective-permute-start.27
  1099.0 23.5 collective-permute-done.24
  1178.6 69.1 %while.23 = (s32[]{:T(128)}, bf16[6,3,564,64]{2,3,0,1:T(8,128)(2,1)}, s32[564]{0:T(1024)S(1)}, bf16[6,564,64]{2,1,0:T(8,128)(2,1)}, bf16[6,564,64]{2,1,0:T(8,128...) while((s32[]{:T(128)}, ...), condition=%wide.region_27.28_spmd, body=%wide.region_25.27_spmd.sunk | while | flops 207346144 | bytes 8020453 | solution.py:330
  1290.3 14.8 pad_maximum_fusion.1
  1305.1 28.4 copy.159
  1359.7 10.8 maximum_bitcast_fusion.1
  1370.6 21.0 pad_maximum_fusion
  1391.6 55.7 %copy.161 = f32[1536,2,3072]{2,1,0:T(2,128)} copy(f32[1536,2,3072]{0,2,1:T(8,128)} %pad_maximum_fusion) | data formatting | bytes 75497472 | tf_op jit(solution)/shard_map/stack | solution.py:173
  1466.0 33.1 %all-gather.3 = f32[16,2,6,384]{3,1,2,0:T(2,128)S(1)} all-gather(f32[2,2,6,384]{3,1,2,0:T(2,128)S(1)} %copy.155), channel_id=5, replica_groups=mesh['row'=8,'col'=4] {'row'}, dimensions={0}, use_global_device_ids=true | all-gather | bytes 331776 | tf_op jit(solution)/shard_map/all_gather | solution.py:359
  1501.3 12.5 all-reduce.3
  1524.7 377.2 %all-reduce.13.cloned.1.call-done = f32[1536,2,1536]{2,1,0:T(2,128)} async-done(((f32[1536,2,1536]{2,1,0:T(2,128)}), f32[1536,2,1536]{2,1,0:T(2,128)}) %all-reduce.13.cloned.1.call-update) | async-done | bytes 18874384
  1907.7 1118.8 %all-reduce.15.cloned.1.call-done = f32[1536,2,3072]{2,1,0:T(2,128)} async-done(((f32[1536,2,3072]{2,1,0:T(2,128)}), f32[1536,2,3072]{2,1,0:T(2,128)}) %all-reduce.15.cloned.1.call-update) | async-done | bytes 37748752
  (489 shorter events, 559.2 us)
Async XLA Ops:
  7.2 89.0 %all-reduce.11.cloned.1.call-start = ((), (), s32[]{:S(2)}) async-start(), calls=%async_computation.16 | async-start | bytes 589824
  10.5 202.0 %all-gather.15.cloned.1.call-start = ((), (), s32[]{:S(2)}) async-start(), calls=%async_computation.5 | async-start | bytes 7962624 | tf_op jit(solution)/shard_map/all_gather | solution.py:148
  14.3 219.2 %all-gather.13.cloned.1.call-start = ((), (), s32[]{:S(2)}) async-start(), calls=%async_computation.4 | async-start | bytes 2181120 | tf_op jit(solution)/shard_map/all_gather | solution.py:123
  17.4 82.4 %collective-permute-start.4 = (bf16[192,2,384]{2,1,0:T(2,128)(2,1)}, bf16[192,2,384]{2,1,0:T(2,128)(2,1)}, u32[]{:S(2)}, u32[]{:S(2)}) collective-permute-start(bf16[192,2,384]{2,1,0:T(2,128)(2,1)} %bitcast.415), channel_id=1, source_target_pairs={{4,0},{8,4},{12,8},{16,12},{20,16},{24,20},{28,24},{0,28},{5,1},{9... | collective-permute-start | bytes 884744 | tf_op jit(solution)/shard_map/ppermute | solution.py:33
  31.3 66.4 %collective-permute-start.1 = (bf16[192,2,384]{2,1,0:T(2,128)(2,1)}, bf16[192,2,384]{2,1,0:T(2,128)(2,1)}, u32[]{:S(2)}, u32[]{:S(2)}) collective-permute-start(bf16[192,2,384]{2,1,0:T(2,128)(2,1)} %collective-permute-done), channel_id=1, source_target_pairs={{0,4},{4,8},{8,12},{12,16},{16,20},{20,24},{24,28},{28,0},{1,5},{5... | collective-permute-start | bytes 884744 | tf_op jit(solution)/shard_map/ppermute | solution.py:30
  123.7 499.4 %reduce-scatter.6.cloned.1.call-start = ((), (), s32[]{:S(2)}) async-start(), calls=%async_computation.6 | async-start | bytes 4362240 | tf_op jit(solution)/shard_map/reduce_scatter | solution.py:131
  276.8 421.7 %all-gather.19.cloned.1.call-start = ((), (), s32[]{:S(2)}) async-start(), calls=%async_computation.9 | async-start | bytes 2181120 | tf_op jit(solution)/shard_map/all_gather | solution.py:127
  281.9 416.6 %all-gather.25.cloned.1.call-start = ((), (), s32[]{:S(2)}) async-start(), calls=%async_computation.14 | async-start | bytes 10616832 | tf_op jit(solution)/shard_map/all_gather | solution.py:148
  284.4 516.0 %all-gather.23.cloned.1.call-start = ((), (), s32[]{:S(2)}) async-start(), calls=%async_computation.13 | async-start | bytes 10616832 | tf_op jit(solution)/shard_map/all_gather | solution.py:148
  285.7 535.7 %all-gather.17.cloned.1.call-start = ((), (), s32[]{:S(2)}) async-start(), calls=%async_computation.7 | async-start | bytes 2181120 | tf_op jit(solution)/shard_map/all_gather | solution.py:123
  316.6 64.3 %collective-permute-start.15 = (bf16[192,2,1536]{2,1,0:T(2,128)(2,1)S(1)}, bf16[192,2,1536]{2,1,0:T(2,128)(2,1)}, u32[]{:S(2)}, u32[]{:S(2)}) collective-permute-start(bf16[192,2,1536]{2,1,0:T(2,128)(2,1)S(1)} %collective-permute-done.14), channel_id=1, source_target_pairs={{0,4},{4,8},{8,12},{12,16},{16,20},{20,24},{24,28},{28,0},{1,5},{5... | collective-permute-start | bytes 3538952 | tf_op jit(solution)/shard_map/ppermute | solution.py:30
  316.6 114.9 %collective-permute-start.7 = (bf16[192,2,1536]{2,1,0:T(2,128)(2,1)}, bf16[192,2,1536]{2,1,0:T(2,128)(2,1)}, u32[]{:S(2)}, u32[]{:S(2)}) collective-permute-start(bf16[192,2,1536]{2,1,0:T(2,128)(2,1)} %bitcast.394), channel_id=1, source_target_pairs={{0,4},{4,8},{8,12},{12,16},{16,20},{20,24},{24,28},{28,0},{1,5},{5... | collective-permute-start | bytes 3538952 | tf_op jit(solution)/shard_map/ppermute | solution.py:30
  317.9 116.1 %collective-permute-start.18 = (bf16[192,2,1536]{2,1,0:T(2,128)(2,1)S(1)}, bf16[192,2,1536]{2,1,0:T(2,128)(2,1)}, u32[]{:S(2)}, u32[]{:S(2)}) collective-permute-start(bf16[192,2,1536]{2,1,0:T(2,128)(2,1)S(1)} %bitcast.393), channel_id=1, source_target_pairs={{4,0},{8,4},{12,8},{16,12},{20,16},{24,20},{28,24},{0,28},{5,1},{9... | collective-permute-start | bytes 3538952 | tf_op jit(solution)/shard_map/ppermute | solution.py:33
  380.8 125.1 %collective-permute-start.16 = (bf16[192,2,1536]{2,1,0:T(2,128)(2,1)}, bf16[192,2,1536]{2,1,0:T(2,128)(2,1)}, u32[]{:S(2)}, u32[]{:S(2)}) collective-permute-start(bf16[192,2,1536]{2,1,0:T(2,128)(2,1)} %collective-permute-done.15), channel_id=1, source_target_pairs={{0,4},{4,8},{8,12},{12,16},{16,20},{20,24},{24,28},{28,0},{1,5},{5... | collective-permute-start | bytes 3538952 | tf_op jit(solution)/shard_map/ppermute | solution.py:30
  383.4 455.9 %collective-permute-start.11 = (bf16[192,2,1536]{2,1,0:T(2,128)(2,1)}, bf16[192,2,1536]{2,1,0:T(2,128)(2,1)}, u32[]{:S(2)}, u32[]{:S(2)}) collective-permute-start(bf16[192,2,1536]{2,1,0:T(2,128)(2,1)} %bitcast.395), channel_id=1, source_target_pairs={{4,0},{8,4},{12,8},{16,12},{20,16},{24,20},{28,24},{0,28},{5,1},{9... | collective-permute-start | bytes 3538952 | tf_op jit(solution)/shard_map/ppermute | solution.py:33
  431.5 125.0 %collective-permute-start.8 = (bf16[192,2,1536]{2,1,0:T(2,128)(2,1)}, bf16[192,2,1536]{2,1,0:T(2,128)(2,1)}, u32[]{:S(2)}, u32[]{:S(2)}) collective-permute-start(bf16[192,2,1536]{2,1,0:T(2,128)(2,1)} %collective-permute-done.7), channel_id=1, source_target_pairs={{0,4},{4,8},{8,12},{12,16},{16,20},{20,24},{24,28},{28,0},{1,5},{5... | collective-permute-start | bytes 3538952 | tf_op jit(solution)/shard_map/ppermute | solution.py:30
  434.0 177.1 %collective-permute-start.19 = (bf16[192,2,1536]{2,1,0:T(2,128)(2,1)}, bf16[192,2,1536]{2,1,0:T(2,128)(2,1)}, u32[]{:S(2)}, u32[]{:S(2)}) collective-permute-start(bf16[192,2,1536]{2,1,0:T(2,128)(2,1)} %collective-permute-done.18), channel_id=1, source_target_pairs={{4,0},{8,4},{12,8},{16,12},{20,16},{24,20},{28,24},{0,28},{5,1},{9... | collective-permute-start | bytes 3538952 | tf_op jit(solution)/shard_map/ppermute | solution.py:33
  505.9 105.2 %collective-permute-start.17 = (bf16[192,2,1536]{2,1,0:T(2,128)(2,1)}, bf16[192,2,1536]{2,1,0:T(2,128)(2,1)S(1)}, u32[]{:S(2)}, u32[]{:S(2)}) collective-permute-start(bf16[192,2,1536]{2,1,0:T(2,128)(2,1)} %collective-permute-done.16), channel_id=1, source_target_pairs={{0,4},{4,8},{8,12},{12,16},{16,20},{20,24},{24,28},{28,0},{1,5},{5... | collective-permute-start | bytes 3538952 | tf_op jit(solution)/shard_map/ppermute | solution.py:30
  556.5 287.1 %collective-permute-start.9 = (bf16[192,2,1536]{2,1,0:T(2,128)(2,1)}, bf16[192,2,1536]{2,1,0:T(2,128)(2,1)}, u32[]{:S(2)}, u32[]{:S(2)}) collective-permute-start(bf16[192,2,1536]{2,1,0:T(2,128)(2,1)} %collective-permute-done.8), channel_id=1, source_target_pairs={{0,4},{4,8},{8,12},{12,16},{16,20},{20,24},{24,28},{28,0},{1,5},{5... | collective-permute-start | bytes 3538952 | tf_op jit(solution)/shard_map/ppermute | solution.py:30
  611.1 50.6 %collective-permute-start.20 = (bf16[192,2,1536]{2,1,0:T(2,128)(2,1)}, bf16[192,2,1536]{2,1,0:T(2,128)(2,1)}, u32[]{:S(2)}, u32[]{:S(2)}) collective-permute-start(bf16[192,2,1536]{2,1,0:T(2,128)(2,1)} %collective-permute-done.19), channel_id=1, source_target_pairs={{4,0},{8,4},{12,8},{16,12},{20,16},{24,20},{28,24},{0,28},{5,1},{9... | collective-permute-start | bytes 3538952 | tf_op jit(solution)/shard_map/ppermute | solution.py:33
  633.3 495.8 %reduce-scatter.10.cloned.1.call-start = ((), (), s32[]{:S(2)}) async-start(), calls=%async_computation.10 | async-start | bytes 4362240 | tf_op jit(solution)/shard_map/reduce_scatter | solution.py:135
  839.2 297.6 %reduce-scatter.8.cloned.1.call-start = ((), (), s32[]{:S(2)}) async-start(), calls=%async_computation.8 | async-start | bytes 4362240 | tf_op jit(solution)/shard_map/reduce_scatter | solution.py:131
  839.3 53.6 %collective-permute-start.12 = (bf16[192,2,1536]{2,1,0:T(2,128)(2,1)}, bf16[192,2,1536]{2,1,0:T(2,128)(2,1)S(1)}, u32[]{:S(2)}, u32[]{:S(2)}) collective-permute-start(bf16[192,2,1536]{2,1,0:T(2,128)(2,1)} %collective-permute-done.11), channel_id=1, source_target_pairs={{4,0},{8,4},{12,8},{16,12},{20,16},{24,20},{28,24},{0,28},{5,1},{9... | collective-permute-start | bytes 3538952 | tf_op jit(solution)/shard_map/ppermute | solution.py:33
  843.6 52.0 %collective-permute-start.10 = (bf16[192,2,1536]{2,1,0:T(2,128)(2,1)}, bf16[192,2,1536]{2,1,0:T(2,128)(2,1)S(1)}, u32[]{:S(2)}, u32[]{:S(2)}) collective-permute-start(bf16[192,2,1536]{2,1,0:T(2,128)(2,1)} %collective-permute-done.9), channel_id=1, source_target_pairs={{0,4},{4,8},{8,12},{12,16},{16,20},{20,24},{24,28},{28,0},{1,5},{5... | collective-permute-start | bytes 3538952 | tf_op jit(solution)/shard_map/ppermute | solution.py:30
  966.3 200.5 %all-gather.27.cloned.1.call-start = ((), (), s32[]{:S(2)}) async-start(), calls=%async_computation.15 | async-start | bytes 2654208 | tf_op jit(solution)/shard_map/all_gather | solution.py:148
  1031.6 142.1 %all-gather.21.cloned.1.call-start = ((), (), s32[]{:S(2)}) async-start(), calls=%async_computation.11 | async-start | bytes 2181120 | tf_op jit(solution)/shard_map/all_gather | solution.py:127
  1031.6 44.8 %collective-permute-start.26 = (bf16[192,2,1152]{2,0,1:T(8,128)(2,1)}, bf16[192,2,1152]{2,0,1:T(8,128)(2,1)}, u32[]{:S(2)}, u32[]{:S(2)}) collective-permute-start(bf16[192,2,1152]{2,0,1:T(8,128)(2,1)} %collective-permute-done.25), channel_id=1, source_target_pairs={{4,0},{8,4},{12,8},{16,12},{20,16},{24,20},{28,24},{0,28},{5,1},{9... | collective-permute-start | bytes 2654216 | tf_op jit(solution)/shard_map/ppermute | solution.py:33
  1070.6 51.9 %collective-permute-start.24 = (bf16[192,2,1152]{2,0,1:T(8,128)(2,1)}, bf16[192,2,1152]{2,0,1:T(8,128)(2,1)}, u32[]{:S(2)}, u32[]{:S(2)}) collective-permute-start(bf16[192,2,1152]{2,0,1:T(8,128)(2,1)} %collective-permute-done.23), channel_id=1, source_target_pairs={{0,4},{4,8},{8,12},{12,16},{16,20},{20,24},{24,28},{28,0},{1,5},{5... | collective-permute-start | bytes 2654216 | tf_op jit(solution)/shard_map/ppermute | solution.py:30
  1076.4 74.4 %collective-permute-start.27 = (bf16[192,2,1152]{2,0,1:T(8,128)(2,1)}, bf16[192,2,1152]{2,0,1:T(8,128)(2,1)}, u32[]{:S(2)}, u32[]{:S(2)}) collective-permute-start(bf16[192,2,1152]{2,0,1:T(8,128)(2,1)} %collective-permute-done.26), channel_id=1, source_target_pairs={{4,0},{8,4},{12,8},{16,12},{20,16},{24,20},{28,24},{0,28},{5,1},{9... | collective-permute-start | bytes 2654216 | tf_op jit(solution)/shard_map/ppermute | solution.py:33
  1143.1 315.8 %reduce-scatter.12.cloned.1.call-start = ((), (), s32[]{:S(2)}) async-start(), calls=%async_computation.12 | async-start | bytes 4362240 | tf_op jit(solution)/shard_map/reduce_scatter | solution.py:135
  1259.4 642.4 %all-reduce.13.cloned.1.call-start = ((), (), s32[]{:S(2)}) async-start(), calls=%async_computation.17 | async-start | bytes 37748736
  1333.6 1693.0 %all-reduce.15.cloned.1.call-start = ((), (), s32[]{:S(2)}) async-start(), calls=%async_computation.18 | async-start | bytes 75497472
  (80 other events, 3159.8 us)
Sparse Core Ops, SparseCore 0:
  11.9 84.2 all-reduce.10
  98.4 114.1 all-gather.14
  214.7 18.7 all-gather.12
  276.9 39.8 reduce-scatter.5
  318.2 20.5 all-gather.18
  341.4 320.2 all-gather.24
  664.6 135.7 all-gather.22
  802.5 18.7 all-gather.16
  839.3 39.8 reduce-scatter.9
  966.5 40.7 reduce-scatter.7
  1031.7 94.6 all-gather.26
  1143.2 18.8 all-gather.20
  1259.6 37.9 reduce-scatter.11
  1333.7 568.1 all-reduce.12
  1906.0 1120.5 all-reduce.14
